TPU v7x, 256 devices: a whole 4x4x8 slice. The times are simulated.
256 devices in a mesh: freq: 16 (over y, x), param: 4 (over z_hi, core), sens: 4 (over z_lo).
Axes of the slice: x: 4, y: 4, z: 8 (z_hi: 2, z_lo: 4; z = z_hi * 4 + z_lo), core: 2. Of those that a mesh axis runs over, the one named last changes fastest.
Arguments:
- series: bfloat16 [8, 600, 416], P(None, 'sens', 'freq'), may hold values from -6 to 6
- kernel: bfloat16 [2, 256, 600, 4096], P(None, 'freq', 'sens', 'param'), may hold values from -0.1875 to 0.1875
- prior_spectrum: float32 [256], P('freq'), may hold values from 0.3 to 1.5
- prior_scale: float32 [4096], P('param'), may hold values from 0.5 to 2
Outputs:
- adjoint_map: float32 [416, 8, 4096], P('freq', 'sens', 'param')
All inputs are finite; a program needn't handle non-finite values.
Results may differ from a plain program's by a relative error of at most 0.0047.
Values may be sent and summed in bfloat16 or wider, within the bound.
A program may use at most 64 MiB of HBM per device.

v0:
```python
import math
import jax
import jax.numpy as jnp
from jax import lax
from jax.sharding import PartitionSpec as P

LEN = 840
FB_DEV = 16


def joined_along(blocks, dim):
    blocks = jnp.moveaxis(blocks, 0, dim)
    lengths = blocks.shape
    return blocks.reshape(*lengths[:dim], lengths[dim] * lengths[dim + 1], *lengths[dim + 2 :])


def copy_for_each(x, axis):
    copies = jnp.broadcast_to(x, (lax.axis_size(axis), *x.shape))
    return lax.all_to_all(copies, axis, split_axis=0, concat_axis=0, tiled=True)


def gather_directly(x, axis, dim):
    return joined_along(copy_for_each(x, axis), dim)


def in_blocks(x, dim, count):
    before, after = (x.shape[:dim], x.shape[dim + 1 :])
    return jnp.moveaxis(x.reshape(*before, count, -1, *after), dim, 0)


def sent_and_summed(x, axis, dim):
    count = lax.axis_size(axis)
    blocks = lax.all_to_all(in_blocks(x, dim, count), axis, 0, 0, tiled=True)
    return jnp.sum(blocks.astype(jnp.float32), axis=0)


def extended(cells, sides, width):
    for axis, dim in sides:
        count = lax.axis_size(axis)
        ends = count - 1
        head = lax.slice_in_dim(cells, 0, width, axis=dim)
        tail = lax.slice_in_dim(cells, cells.shape[dim] - width, cells.shape[dim], axis=dim)
        cells = jnp.concatenate(
            [
                lax.ppermute(tail, axis, [(i, (i + 1) % count) for i in range(ends)]),
                cells,
                lax.ppermute(head, axis, [((i + 1) % count, i) for i in range(ends)]),
            ],
            axis=dim,
        )
    return cells


def phase_tables(bin_first, bin_count, time_count):
    bin_index = bin_first + jnp.arange(bin_count, dtype=jnp.int32)
    time_index = jnp.arange(time_count, dtype=jnp.int32)
    product = time_index[:, None] * bin_index[None, :] % LEN
    phase_angle = product.astype(jnp.float32) * (2.0 * math.pi / LEN)
    return (jnp.cos(phase_angle), jnp.sin(phase_angle))


def contract(spectrum, operator):
    return jnp.einsum("bsr,bsp->brp", spectrum, operator, preferred_element_type=jnp.float32)


def local(series, kernel, prior_spectrum, prior_scale):
    highest = lax.Precision.HIGHEST
    groups = lax.axis_size("freq")
    first_bin = lax.axis_index("freq") * FB_DEV
    probes, sens_dev, time_dev = series.shape
    total_times = time_dev * groups
    cosine, sine_part = phase_tables(first_bin, FB_DEV, total_times)
    phase_table = jnp.concatenate([cosine, -sine_part], axis=1)
    series_piece = gather_directly(series, "freq", 2)
    row_count = series_piece.shape[2]
    flat_rows = series_piece.astype(jnp.float32).reshape(-1, row_count)
    spectra = jnp.dot(flat_rows, phase_table, precision=highest)
    spectra = (spectra * (1.0 / math.sqrt(total_times))).astype(jnp.bfloat16)
    both_parts = (
        spectra.reshape(probes, sens_dev, 2, FB_DEV)
        .transpose(3, 1, 2, 0)
        .reshape(FB_DEV, sens_dev, 2 * probes)
    )
    with_real = contract(both_parts, kernel[0])
    with_imag = contract(both_parts, kernel[1])
    real_part = with_real[:, :probes] + with_imag[:, probes:]
    imag_part = with_real[:, probes:] - with_imag[:, :probes]
    partial_value = jnp.stack([real_part, imag_part])
    summed = sent_and_summed(partial_value.astype(jnp.bfloat16), "sens", 2)
    weights = prior_spectrum * (1.0 / math.sqrt(FB_DEV * groups))
    scaled_spec = summed * weights[None, :, None, None]
    arrived = lax.all_to_all(scaled_spec, "freq", split_axis=3, concat_axis=1, tiled=True)
    bin_total = arrived.shape[1]
    item_count = arrived.shape[2]
    col_count = arrived.shape[3]
    cos_all, sin_all = phase_tables(0, bin_total, total_times)
    full_table = jnp.concatenate([cos_all, -sin_all], axis=1)
    flat_rows = arrived.reshape(2 * bin_total, item_count * col_count)
    arranged = jnp.dot(full_table, flat_rows, precision=highest).reshape(
        total_times, item_count, col_count
    )
    image_field = lax.all_to_all(arranged, "freq", split_axis=0, concat_axis=2, tiled=True)
    weighted = image_field * prior_scale
    padded = extended(weighted.astype(jnp.bfloat16), (("param", 2),), 1).astype(weighted.dtype)
    smooth = 0.5 * weighted + 0.25 * (padded[:, :, :-2] + padded[:, :, 2:])
    return smooth * prior_scale


def solution(mesh):
    placed = (P(None, "sens", "freq"), P(None, "freq", "sens", "param"), P("freq"), P("param"))
    return jax.shard_map(
        local, mesh=mesh, in_specs=placed, out_specs=P("freq", "sens", "param"), check_vma=False
    )
```

profile of v0, /device:TPU:1, one launch (start us, length us, event | category | flops | bytes accessed | tf_op | source)
XLA Modules:
  0.0 131.3 jit_solution(14938299021006991970)
XLA Ops:
  0.0 2.2 %broadcast_in_dim.2 = bf16[16,8,150,26]{2,1,3,0:T(8,128)(2,1)} broadcast(bf16[8,150,26]{1,0,2:T(8,128)(2,1)} %param.4), dimensions={1,2,3} | broadcast | bytes 1060800 | tf_op jit(solution)/shard_map/broadcast_in_dim | solution.py:18
  2.2 7.6 %all-to-all-start = ((bf16[16,8,150,26]{2,1,3,0:T(8,128)(2,1)}), bf16[16,8,150,26]{2,1,3,0:T(8,128)(2,1)S(1)}, u32[]{:S(2)}, u32[]{:S(2)}) async-start(bf16[16,8,150,26]{2,1,3,0:T(8,128)(2,1)} %broadcast_in_dim.2), calls=%async_computation | async-start | bytes 3407872 | tf_op jit(solution)/shard_map/all_to_all | solution.py:19
  9.8 0.2 fusion.29
  10.0 9.9 %fusion.33 = (bf16[1,16,150,1024]{3,1,2,0:T(8,128)(2,1)}, bf16[1,16,150,1024]{3,1,2,0:T(8,128)(2,1)}) fusion(bf16[2,16,150,1024]{3,1,2,0:T(8,128)(2,1)} %param.5), kind=kLoop, calls=%fused_computation.53 | loop fusion | bytes 19660800 | tf_op jit(solution)/shard_map/slice | solution.py:84
  20.0 14.8 %all-to-all-done = bf16[16,8,150,26]{2,1,3,0:T(8,128)(2,1)S(1)} async-done(((bf16[16,8,150,26]{2,1,3,0:T(8,128)(2,1)}), bf16[16,8,150,26]{2,1,3,0:T(8,128)(2,1)S(1)}, u32[]{:S(2)}, u32[]{:S(2)}) %all-to-all-start) | async-done | bytes 998432 | tf_op jit(solution)/shard_map/all_to_all | solution.py:19
  34.8 1.9 %reshape.30 = bf16[1200,416]{0,1:T(8,128)(2,1)S(1)} reshape(bf16[8,150,16,26]{1,0,3,2:T(8,128)(2,1)S(1)} %bitcast.47) | data formatting | bytes 1996800 | tf_op jit(solution)/shard_map/reshape | solution.py:76
  36.8 0.5 fusion.3
  37.3 0.2 reshape.31
  37.5 0.0 copy-start
  37.5 8.0 %fusion.1 = f32[16,16,1024]{2,1,0:T(8,128)S(1)} fusion(bf16[1,16,150,1024]{3,1,2,0:T(8,128)(2,1)} %get-tuple-element.5, bf16[8,150,2,16]{1,0,3,2:T(8,128)(2,1)S(1)} %reshape.31), kind=kOutput, calls=%fused_computation.3 | convolution fusion | flops 78643200 | bytes 6040576 | tf_op jit(solution)/shard_map/bsr,bsp->brp/dot_general | solution.py:63
  45.5 0.0 copy-done
  45.5 0.0 copy-start.2
  45.5 5.4 %fusion = f32[16,16,1024]{2,1,0:T(8,128)S(1)} fusion(bf16[1,16,150,1024]{3,1,2,0:T(8,128)(2,1)S(1)} %copy-done, bf16[8,150,2,16]{1,0,3,2:T(8,128)(2,1)S(1)} %reshape.31), kind=kOutput, calls=%fused_computation.1 | convolution fusion | flops 78643200 | bytes 6040576 | tf_op jit(solution)/shard_map/bsr,bsp->brp/dot_general | solution.py:63
  50.9 0.2 fusion.8
  51.1 0.1 stack.10
  51.2 0.3 stack.9
  51.6 1.3 %copy_bitcast_fusion.4 = bf16[4,2,16,2,1024]{4,3,2,1,0:T(2,128)(2,1)} fusion(bf16[1,16,4,2,1024]{4,3,2,1,0:T(2,128)(2,1)S(1)} %stack.10, bf16[1,16,4,2,1024]{4,3,2,1,0:T(2,128)(2,1)S(1)} %stack.9), kind=kLoop, calls=%fused_computation.18 | loop fusion | flops 262144 | bytes 1048576 | tf_op jit(solution)/shard_map/transpose | solution.py:28
  52.9 5.6 %all-to-all-start.1 = ((bf16[4,2,16,2,1024]{4,3,2,1,0:T(2,128)(2,1)}), bf16[4,2,16,2,1024]{4,3,2,1,0:T(2,128)(2,1)S(1)}, u32[]{:S(2)}, u32[]{:S(2)}) async-start(bf16[4,2,16,2,1024]{4,3,2,1,0:T(2,128)(2,1)} %copy_bitcast_fusion.4), calls=%async_computation.1 | async-start | bytes 1048576 | tf_op jit(solution)/shard_map/all_to_all | solution.py:33
  58.5 0.0 copy-done.2
  58.5 13.3 %all-to-all-done.1 = bf16[4,2,16,2,1024]{4,3,2,1,0:T(2,128)(2,1)S(1)} async-done(((bf16[4,2,16,2,1024]{4,3,2,1,0:T(2,128)(2,1)}), bf16[4,2,16,2,1024]{4,3,2,1,0:T(2,128)(2,1)S(1)}, u32[]{:S(2)}, u32[]{:S(2)}) %all-to-all-start.1) | async-done | bytes 524320 | tf_op jit(solution)/shard_map/all_to_all | solution.py:33
  71.8 0.1 convert_reduce_fusion
  71.9 0.1 broadcast_multiply_fusion
  72.0 1.3 %copy.43 = f32[2,16,2,1024]{1,2,0,3:T(2,128)S(1)} copy(f32[2,16,2,1024]{3,1,2,0:T(8,128)S(1)} %broadcast_multiply_fusion) | data formatting | bytes 524288 | tf_op jit(solution)/shard_map/mul | solution.py:91
  73.3 3.6 %reshape.35 = f32[16,1,4096]{2,1,0:T(1,128)} reshape(f32[1024,2,2,16]{3,2,1,0:T(2,128)S(1)} %bitcast.46) | data formatting | bytes 524288
  76.9 5.1 %all-to-all-start.2 = ((f32[16,1,4096]{2,1,0:T(1,128)}), f32[16,1,4096]{2,1,0:T(1,128)S(1)}, u32[]{:S(2)}, u32[]{:S(2)}) async-start(f32[16,1,4096]{2,1,0:T(1,128)} %reshape.35), calls=%async_computation.2 | async-start | bytes 524288 | tf_op jit(solution)/shard_map/all_to_all | solution.py:92
  82.1 1.8 %sine_negate_fusion = (f32[416,256]{1,0:T(8,128)S(1)}, f32[416,256]{1,0:T(8,128)S(1)}) fusion(), kind=kLoop, calls=%fused_computation.21 | loop fusion | flops 1064960 | bytes 851968 | tf_op jit(solution)/shard_map/neg | solution.py:97
  83.9 5.9 %all-to-all-done.2 = f32[16,1,4096]{2,1,0:T(1,128)S(1)} async-done(((f32[16,1,4096]{2,1,0:T(1,128)}), f32[16,1,4096]{2,1,0:T(1,128)S(1)}, u32[]{:S(2)}, u32[]{:S(2)}) %all-to-all-start.2) | async-done | bytes 262176 | tf_op jit(solution)/shard_map/all_to_all | solution.py:92
  89.7 0.5 broadcast.17
  90.2 1.3 reduce
  91.5 2.8 %reshape.36 = f32[1024,2,2,16]{3,2,1,0:T(2,128)S(1)} reshape(f32[16,4096]{1,0:T(8,128)S(1)} %reduce) | data formatting | bytes 524288
  94.3 0.0 copy-start.1
  94.3 1.5 %copy.50 = f32[2,16,2,16,64]{4,3,1,2,0:T(8,128)S(1)} copy(f32[2,16,2,16,64]{1,2,0,4,3:T(2,128)S(1)} %bitcast.45) | data formatting | bytes 524288 | tf_op jit(solution)/shard_map/all_to_all | solution.py:92
  95.9 0.4 copy.45
  96.3 0.3 reshape.33
  96.6 0.1 copy.46
  96.7 0.9 fusion.4
  97.6 0.2 copy.47
  97.9 0.4 reshape.37
  98.3 10.1 %all_to_all.43 = f32[16,1,3328]{2,1,0:T(1,128)S(1)} all-to-all(f32[16,1,3328]{2,1,0:T(1,128)S(1)} %reshape.37), channel_id=1, replica_groups=mesh['freq'=16,'param'=4,'sens'=4] {'freq'}, dimensions={0} | all-to-all | bytes 425984 | tf_op jit(solution)/shard_map/all_to_all | solution.py:102
  108.4 1.1 reduce.1
  109.6 0.3 reshape.38
  109.9 0.2 all_to_all.38
  110.1 0.0 copy-done.1
  110.2 0.1 multiply_convert_fusion
  110.2 0.1 fusion.34
  110.3 10.5 %collective-permute-start = (bf16[26,2,1]{2,1,0:T(2,128)(2,1)S(1)}, bf16[26,2,1]{2,1,0:T(2,128)(2,1)S(1)}, u32[]{:S(2)}, u32[]{:S(2)}) collective-permute-start(bf16[26,2,1]{2,1,0:T(2,128)(2,1)S(1)} %get-tuple-element.10), channel_id=1, source_target_pairs={{0,4},{4,8},{8,12},{1,5},{5,9},{9,13},{2,6},{6,10},{10,14},{3,7},{... | collective-permute-start | bytes 320 | tf_op jit(solution)/shard_map/ppermute | solution.py:45
  120.8 1.9 %collective-permute-start.1 = (bf16[26,2,1]{2,1,0:T(2,128)(2,1)S(1)}, bf16[26,2,1]{2,1,0:T(2,128)(2,1)S(1)}, u32[]{:S(2)}, u32[]{:S(2)}) collective-permute-start(bf16[26,2,1]{2,1,0:T(2,128)(2,1)S(1)} %get-tuple-element.9), channel_id=1, source_target_pairs={{4,0},{8,4},{12,8},{5,1},{9,5},{13,9},{6,2},{10,6},{14,10},{7,3},{... | collective-permute-start | bytes 320 | tf_op jit(solution)/shard_map/ppermute | solution.py:47
  122.8 0.0 collective-permute-done
  122.8 7.0 %collective-permute-done.1 = bf16[26,2,1]{2,1,0:T(2,128)(2,1)S(1)} collective-permute-done((bf16[26,2,1]{2,1,0:T(2,128)(2,1)S(1)}, bf16[26,2,1]{2,1,0:T(2,128)(2,1)S(1)}, u32[]{:S(2)}, u32[]{:S(2)}) %collective-permute-start.1) | collective-permute-done | bytes 136 | tf_op jit(solution)/shard_map/ppermute | solution.py:47
  129.8 0.5 concatenate.13
  130.2 0.1 convert_element_type.32
  130.3 1.0 fusion.17
  (3 shorter events, 0.0 us)
Async XLA Ops:
  2.2 32.6 %all-to-all-start = ((bf16[16,8,150,26]{2,1,3,0:T(8,128)(2,1)}), bf16[16,8,150,26]{2,1,3,0:T(8,128)(2,1)S(1)}, u32[]{:S(2)}, u32[]{:S(2)}) async-start(bf16[16,8,150,26]{2,1,3,0:T(8,128)(2,1)} %broadcast_in_dim.2), calls=%async_computation | async-start | bytes 3407872 | tf_op jit(solution)/shard_map/all_to_all | solution.py:19
  37.5 8.0 %copy-start = (bf16[1,16,150,1024]{3,1,2,0:T(8,128)(2,1)S(1)}, bf16[1,16,150,1024]{3,1,2,0:T(8,128)(2,1)}, u32[]{:S(2)}) copy-start(bf16[1,16,150,1024]{3,1,2,0:T(8,128)(2,1)} %get-tuple-element.6) | copy-start | bytes 14745604
  45.5 13.0 %copy-start.2 = (f32[16]{0:T(128)S(1)}, f32[16]{0:T(128)}, u32[]{:S(2)}) copy-start(f32[16]{0:T(128)} %param.6) | copy-start | bytes 196
  52.9 18.9 %all-to-all-start.1 = ((bf16[4,2,16,2,1024]{4,3,2,1,0:T(2,128)(2,1)}), bf16[4,2,16,2,1024]{4,3,2,1,0:T(2,128)(2,1)S(1)}, u32[]{:S(2)}, u32[]{:S(2)}) async-start(bf16[4,2,16,2,1024]{4,3,2,1,0:T(2,128)(2,1)} %copy_bitcast_fusion.4), calls=%async_computation.1 | async-start | bytes 1048576 | tf_op jit(solution)/shard_map/all_to_all | solution.py:33
  76.9 12.8 %all-to-all-start.2 = ((f32[16,1,4096]{2,1,0:T(1,128)}), f32[16,1,4096]{2,1,0:T(1,128)S(1)}, u32[]{:S(2)}, u32[]{:S(2)}) async-start(f32[16,1,4096]{2,1,0:T(1,128)} %reshape.35), calls=%async_computation.2 | async-start | bytes 524288 | tf_op jit(solution)/shard_map/all_to_all | solution.py:92
  94.3 15.8 %copy-start.1 = (f32[1024]{0:T(1024)S(1)}, f32[1024]{0:T(1024)}, u32[]{:S(2)}) copy-start(f32[1024]{0:T(1024)} %param.7) | copy-start | bytes 12292
  110.3 12.4 %collective-permute-start = (bf16[26,2,1]{2,1,0:T(2,128)(2,1)S(1)}, bf16[26,2,1]{2,1,0:T(2,128)(2,1)S(1)}, u32[]{:S(2)}, u32[]{:S(2)}) collective-permute-start(bf16[26,2,1]{2,1,0:T(2,128)(2,1)S(1)} %get-tuple-element.10), channel_id=1, source_target_pairs={{0,4},{4,8},{8,12},{1,5},{5,9},{9,13},{2,6},{6,10},{10,14},{3,7},{... | collective-permute-start | bytes 320 | tf_op jit(solution)/shard_map/ppermute | solution.py:45
  120.8 8.9 %collective-permute-start.1 = (bf16[26,2,1]{2,1,0:T(2,128)(2,1)S(1)}, bf16[26,2,1]{2,1,0:T(2,128)(2,1)S(1)}, u32[]{:S(2)}, u32[]{:S(2)}) collective-permute-start(bf16[26,2,1]{2,1,0:T(2,128)(2,1)S(1)} %get-tuple-element.9), channel_id=1, source_target_pairs={{4,0},{8,4},{12,8},{5,1},{9,5},{13,9},{6,2},{10,6},{14,10},{7,3},{... | collective-permute-start | bytes 320 | tf_op jit(solution)/shard_map/ppermute | solution.py:47
where the time goes:
time: 132 us; the launch traced here: 131 us
  waiting for transfers between devices  41 us (31%)
  starting transfers between devices  30.7 us (23%)
  local copies, waits for them, and re-layouts  27.1 us (21%)
  matrix products  14.8 us (11%)
  blocking collectives  10.1 us (8%)
  other arithmetic  7.26 us (6%)
    all_to_all x1, waiting for transfers between devices, copy_for_each(): return lax.all_to_all(copies, axis, split_axis=0, concat_axis=0, tiled=True)  14.8 us
    dot_general x2, matrix products, contract(): jnp.einsum('bsr,bsp->brp', spectrum, operator, preferred_element_type=jnp...  13.4 us
    all_to_all x1, waiting for transfers between devices, sent_and_summed(): blocks = lax.all_to_all(in_blocks(x, dim, count), axis, 0, 0, tiled=True)  13.3 us
    ppermute x1, starting transfers between devices, extended(): lax.ppermute(tail, axis, [(i, (i + 1) % count) for i in range(ends)])  10.5 us
    all_to_all x1, blocking collectives, local(): lax.all_to_all(arranged, 'freq', split_axis=0, concat_axis=2, tiled=True)  10.1 us
    slice x1, local copies, waits for them, and re-layouts, local(): with_real = contract(both_parts, kernel[0])  9.95 us
    all_to_all x1, starting transfers between devices, copy_for_each(): return lax.all_to_all(copies, axis, split_axis=0, concat_axis=0, tiled=True)  7.57 us
    unnamed x10, local copies, waits for them, and re-layouts  7.13 us
  transfers between devices with their start and end apart: 5, of which 4 were waited for; matrix products, arithmetic and copies ran while one was open for 9% of the time, Pallas kernels for 0%

commit v1 on v0

--- a/solution.py
+++ b/solution.py
@@ -89,7 +89,12 @@
     summed = sent_and_summed(partial_value.astype(jnp.bfloat16), "sens", 2)
     weights = prior_spectrum * (1.0 / math.sqrt(FB_DEV * groups))
     scaled_spec = summed * weights[None, :, None, None]
-    arrived = lax.all_to_all(scaled_spec, "freq", split_axis=3, concat_axis=1, tiled=True)
+    arrived = jnp.concatenate(
+        lax.all_to_all(
+            jnp.stack(jnp.split(scaled_spec, lax.axis_size("freq"), axis=3)), "freq", 0, 0
+        ),
+        axis=1,
+    )
     bin_total = arrived.shape[1]
     item_count = arrived.shape[2]
     col_count = arrived.shape[3]

time: 132 us -> 125 us (0.947)
  local copies, waits for them, and re-layouts: 27.1 us -> 20.2 us
    unnamed x10 -> x25, local copies, waits for them, and re-layouts: 7.13 us -> 3.34 us
    all_to_all x3 -> x1, local copies, waits for them, and re-layouts: 2.46 us -> 0.51 us  [local(): lax.all_to_all(jnp.stack(jnp.split(scaled_spec, lax.axis_size('freq'), ax...]
    mul x1 -> x0, local copies, waits for them, and re-layouts: 1.35 us -> none  [local(): scaled_spec = summed * weights[None, :, None, None]]
  transfers between devices with their start and end apart: 5 -> 5, of which waited for: 4 -> 4; matrix products, arithmetic and copies ran while one was open for 9% -> 10% of each run, Pallas kernels for 0% -> 0%
where the time goes in v1:
time: 125 us
  waiting for transfers between devices  41 us (33%)
  starting transfers between devices  30.7 us (25%)
  local copies, waits for them, and re-layouts  20.2 us (16%)
  matrix products  14.8 us (12%)
  blocking collectives  10.1 us (8%)
  other arithmetic  7.74 us (6%)
    all_to_all x1, waiting for transfers between devices, copy_for_each(): return lax.all_to_all(copies, axis, split_axis=0, concat_axis=0, tiled=True)  14.8 us
    dot_general x2, matrix products, contract(): jnp.einsum('bsr,bsp->brp', spectrum, operator, preferred_element_type=jnp...  13.4 us
    all_to_all x1, waiting for transfers between devices, sent_and_summed(): blocks = lax.all_to_all(in_blocks(x, dim, count), axis, 0, 0, tiled=True)  13.3 us
    ppermute x1, starting transfers between devices, extended(): lax.ppermute(tail, axis, [(i, (i + 1) % count) for i in range(ends)])  10.5 us
    all_to_all x1, blocking collectives, local(): lax.all_to_all(arranged, 'freq', split_axis=0, concat_axis=2, tiled=True)  10.1 us
    slice x1, local copies, waits for them, and re-layouts, local(): with_real = contract(both_parts, kernel[0])  9.95 us
    all_to_all x1, starting transfers between devices, copy_for_each(): return lax.all_to_all(copies, axis, split_axis=0, concat_axis=0, tiled=True)  7.57 us
    ppermute x1, waiting for transfers between devices, extended(): lax.ppermute(head, axis, [((i + 1) % count, i) for i in range(ends)])  6.99 us
  transfers between devices with their start and end apart: 5, of which 4 were waited for; matrix products, arithmetic and copies ran while one was open for 10% of the time, Pallas kernels for 0%

profile of v1, /device:TPU:1, one launch (start us, length us, event | category | flops | bytes accessed | tf_op | source)
XLA Modules:
  0.0 124.9 jit_solution(4804011337673413131)
XLA Ops:
  0.0 2.2 %broadcast_in_dim.2 = bf16[16,8,150,26]{2,1,3,0:T(8,128)(2,1)} broadcast(bf16[8,150,26]{1,0,2:T(8,128)(2,1)} %param.4), dimensions={1,2,3} | broadcast | bytes 1060800 | tf_op jit(solution)/shard_map/broadcast_in_dim | solution.py:18
  2.2 7.6 %all-to-all-start = ((bf16[16,8,150,26]{2,1,3,0:T(8,128)(2,1)}), bf16[16,8,150,26]{2,1,3,0:T(8,128)(2,1)S(1)}, u32[]{:S(2)}, u32[]{:S(2)}) async-start(bf16[16,8,150,26]{2,1,3,0:T(8,128)(2,1)} %broadcast_in_dim.2), calls=%async_computation | async-start | bytes 3407872 | tf_op jit(solution)/shard_map/all_to_all | solution.py:19
  9.8 0.2 fusion.29
  10.0 9.9 %fusion.33 = (bf16[1,16,150,1024]{3,1,2,0:T(8,128)(2,1)}, bf16[1,16,150,1024]{3,1,2,0:T(8,128)(2,1)}) fusion(bf16[2,16,150,1024]{3,1,2,0:T(8,128)(2,1)} %param.5), kind=kLoop, calls=%fused_computation.85 | loop fusion | bytes 19660800 | tf_op jit(solution)/shard_map/slice | solution.py:84
  20.0 14.8 %all-to-all-done = bf16[16,8,150,26]{2,1,3,0:T(8,128)(2,1)S(1)} async-done(((bf16[16,8,150,26]{2,1,3,0:T(8,128)(2,1)}), bf16[16,8,150,26]{2,1,3,0:T(8,128)(2,1)S(1)}, u32[]{:S(2)}, u32[]{:S(2)}) %all-to-all-start) | async-done | bytes 998432 | tf_op jit(solution)/shard_map/all_to_all | solution.py:19
  34.8 1.9 %reshape.29 = bf16[1200,416]{0,1:T(8,128)(2,1)S(1)} reshape(bf16[8,150,16,26]{1,0,3,2:T(8,128)(2,1)S(1)} %bitcast.106) | data formatting | bytes 1996800 | tf_op jit(solution)/shard_map/reshape | solution.py:76
  36.8 0.5 fusion.3
  37.3 0.2 reshape.30
  37.5 0.0 copy-start
  37.5 8.0 %fusion.1 = f32[16,16,1024]{2,1,0:T(8,128)S(1)} fusion(bf16[1,16,150,1024]{3,1,2,0:T(8,128)(2,1)} %get-tuple-element.5, bf16[8,150,2,16]{1,0,3,2:T(8,128)(2,1)S(1)} %reshape.30), kind=kOutput, calls=%fused_computation.3 | convolution fusion | flops 78643200 | bytes 6040576 | tf_op jit(solution)/shard_map/bsr,bsp->brp/dot_general | solution.py:63
  45.5 0.0 copy-done
  45.5 0.0 copy-start.2
  45.5 5.4 %fusion = f32[16,16,1024]{2,1,0:T(8,128)S(1)} fusion(bf16[1,16,150,1024]{3,1,2,0:T(8,128)(2,1)S(1)} %copy-done, bf16[8,150,2,16]{1,0,3,2:T(8,128)(2,1)S(1)} %reshape.30), kind=kOutput, calls=%fused_computation.1 | convolution fusion | flops 78643200 | bytes 6040576 | tf_op jit(solution)/shard_map/bsr,bsp->brp/dot_general | solution.py:63
  50.9 0.2 fusion.8
  51.1 0.1 stack.60
  51.2 0.3 stack.61
  51.6 1.3 %copy_bitcast_fusion.4 = bf16[4,2,16,2,1024]{4,3,2,1,0:T(2,128)(2,1)} fusion(bf16[1,16,4,2,1024]{4,3,2,1,0:T(2,128)(2,1)S(1)} %stack.61, bf16[1,16,4,2,1024]{4,3,2,1,0:T(2,128)(2,1)S(1)} %stack.60), kind=kLoop, calls=%fused_computation.18 | loop fusion | flops 262144 | bytes 1048576 | tf_op jit(solution)/shard_map/transpose | solution.py:28
  52.9 5.6 %all-to-all-start.1 = ((bf16[4,2,16,2,1024]{4,3,2,1,0:T(2,128)(2,1)}), bf16[4,2,16,2,1024]{4,3,2,1,0:T(2,128)(2,1)S(1)}, u32[]{:S(2)}, u32[]{:S(2)}) async-start(bf16[4,2,16,2,1024]{4,3,2,1,0:T(2,128)(2,1)} %copy_bitcast_fusion.4), calls=%async_computation.1 | async-start | bytes 1048576 | tf_op jit(solution)/shard_map/all_to_all | solution.py:33
  58.5 0.0 copy-done.2
  58.5 13.3 %all-to-all-done.1 = bf16[4,2,16,2,1024]{4,3,2,1,0:T(2,128)(2,1)S(1)} async-done(((bf16[4,2,16,2,1024]{4,3,2,1,0:T(2,128)(2,1)}), bf16[4,2,16,2,1024]{4,3,2,1,0:T(2,128)(2,1)S(1)}, u32[]{:S(2)}, u32[]{:S(2)}) %all-to-all-start.1) | async-done | bytes 524320 | tf_op jit(solution)/shard_map/all_to_all | solution.py:33
  71.8 0.5 convert_reduce_fusion
  72.3 0.2 broadcast_multiply_fusion
  72.5 0.1 constant_dynamic-update-slice_fusion.14
  72.6 0.1 constant_dynamic-update-slice_fusion.12
  72.8 0.1 constant_dynamic-update-slice_fusion.10
  72.9 0.1 constant_dynamic-update-slice_fusion.8
  73.1 0.1 constant_dynamic-update-slice_fusion.6
  73.2 0.1 constant_dynamic-update-slice_fusion.4
  73.4 0.1 constant_dynamic-update-slice_fusion.2
  73.5 0.1 constant_dynamic-update-slice_fusion
  73.6 1.3 %reshape.34 = f32[16,1,4096]{2,1,0:T(1,128)} reshape(f32[16,2,16,2,64]{4,3,2,1,0:T(2,128)S(1)} %constant_dynamic-update-slice_fusion) | data formatting | bytes 524288
  74.9 5.1 %all-to-all-start.2 = ((f32[16,1,4096]{2,1,0:T(1,128)}), f32[16,1,4096]{2,1,0:T(1,128)S(1)}, u32[]{:S(2)}, u32[]{:S(2)}) async-start(f32[16,1,4096]{2,1,0:T(1,128)} %reshape.34), calls=%async_computation.2 | async-start | bytes 524288 | tf_op jit(solution)/shard_map/all_to_all | solution.py:93
  80.0 0.0 copy-start.1
  80.0 1.8 %sine_negate_fusion = (f32[416,256]{1,0:T(8,128)S(1)}, f32[416,256]{1,0:T(8,128)S(1)}) fusion(), kind=kLoop, calls=%fused_computation.21 | loop fusion | flops 1064960 | bytes 851968 | tf_op jit(solution)/shard_map/neg | solution.py:102
  81.8 5.8 %all-to-all-done.2 = f32[16,1,4096]{2,1,0:T(1,128)S(1)} async-done(((f32[16,1,4096]{2,1,0:T(1,128)}), f32[16,1,4096]{2,1,0:T(1,128)S(1)}, u32[]{:S(2)}, u32[]{:S(2)}) %all-to-all-start.2) | async-done | bytes 262176 | tf_op jit(solution)/shard_map/all_to_all | solution.py:93
  87.7 0.5 broadcast.17
  88.2 1.3 %reduce = f32[16,4096]{1,0:T(8,128)S(1)} reduce(f32[16,1,4096]{2,1,0:T(1,128)S(1)} %all-to-all-done.2, f32[]{:T(128)} %broadcast.17), dimensions={1}, to_apply=%all_to_all.24.reduce_sub_computation | reduce | bytes 524292 | tf_op jit(solution)/shard_map/all_to_all | solution.py:93
  89.4 0.4 reshape.35
  89.9 0.3 reshape_reshape.3
  90.2 0.1 copy.72
  90.3 0.9 fusion.4
  91.3 0.2 copy.73
  91.5 0.4 reshape.36
  91.9 10.1 %all_to_all.33 = f32[16,1,3328]{2,1,0:T(1,128)S(1)} all-to-all(f32[16,1,3328]{2,1,0:T(1,128)S(1)} %reshape.36), channel_id=1, replica_groups=mesh['freq'=16,'param'=4,'sens'=4] {'freq'}, dimensions={0} | all-to-all | bytes 425984 | tf_op jit(solution)/shard_map/all_to_all | solution.py:107
  102.0 1.1 reduce.1
  103.2 0.3 reshape.37
  103.5 0.2 all_to_all.28
  103.8 0.0 copy-done.1
  103.8 0.1 multiply_convert_fusion
  103.9 0.1 fusion.34
  103.9 10.5 %collective-permute-start = (bf16[26,2,1]{2,1,0:T(2,128)(2,1)S(1)}, bf16[26,2,1]{2,1,0:T(2,128)(2,1)S(1)}, u32[]{:S(2)}, u32[]{:S(2)}) collective-permute-start(bf16[26,2,1]{2,1,0:T(2,128)(2,1)S(1)} %get-tuple-element.10), channel_id=1, source_target_pairs={{0,4},{4,8},{8,12},{1,5},{5,9},{9,13},{2,6},{6,10},{10,14},{3,7},{... | collective-permute-start | bytes 320 | tf_op jit(solution)/shard_map/ppermute | solution.py:45
  114.4 1.9 %collective-permute-start.1 = (bf16[26,2,1]{2,1,0:T(2,128)(2,1)S(1)}, bf16[26,2,1]{2,1,0:T(2,128)(2,1)S(1)}, u32[]{:S(2)}, u32[]{:S(2)}) collective-permute-start(bf16[26,2,1]{2,1,0:T(2,128)(2,1)S(1)} %get-tuple-element.9), channel_id=1, source_target_pairs={{4,0},{8,4},{12,8},{5,1},{9,5},{13,9},{6,2},{10,6},{14,10},{7,3},{... | collective-permute-start | bytes 320 | tf_op jit(solution)/shard_map/ppermute | solution.py:47
  116.4 0.0 collective-permute-done
  116.4 7.0 %collective-permute-done.1 = bf16[26,2,1]{2,1,0:T(2,128)(2,1)S(1)} collective-permute-done((bf16[26,2,1]{2,1,0:T(2,128)(2,1)S(1)}, bf16[26,2,1]{2,1,0:T(2,128)(2,1)S(1)}, u32[]{:S(2)}, u32[]{:S(2)}) %collective-permute-start.1) | collective-permute-done | bytes 136 | tf_op jit(solution)/shard_map/ppermute | solution.py:47
  123.4 0.5 concatenate.13
  123.8 0.1 convert_element_type.32
  123.9 1.0 fusion.17
  (12 shorter events, 0.2 us)
Async XLA Ops:
  2.2 32.6 %all-to-all-start = ((bf16[16,8,150,26]{2,1,3,0:T(8,128)(2,1)}), bf16[16,8,150,26]{2,1,3,0:T(8,128)(2,1)S(1)}, u32[]{:S(2)}, u32[]{:S(2)}) async-start(bf16[16,8,150,26]{2,1,3,0:T(8,128)(2,1)} %broadcast_in_dim.2), calls=%async_computation | async-start | bytes 3407872 | tf_op jit(solution)/shard_map/all_to_all | solution.py:19
  37.5 8.0 %copy-start = (bf16[1,16,150,1024]{3,1,2,0:T(8,128)(2,1)S(1)}, bf16[1,16,150,1024]{3,1,2,0:T(8,128)(2,1)}, u32[]{:S(2)}) copy-start(bf16[1,16,150,1024]{3,1,2,0:T(8,128)(2,1)} %get-tuple-element.6) | copy-start | bytes 14745604
  45.5 13.0 %copy-start.2 = (f32[16]{0:T(128)S(1)}, f32[16]{0:T(128)}, u32[]{:S(2)}) copy-start(f32[16]{0:T(128)} %param.6) | copy-start | bytes 196
  52.9 18.9 %all-to-all-start.1 = ((bf16[4,2,16,2,1024]{4,3,2,1,0:T(2,128)(2,1)}), bf16[4,2,16,2,1024]{4,3,2,1,0:T(2,128)(2,1)S(1)}, u32[]{:S(2)}, u32[]{:S(2)}) async-start(bf16[4,2,16,2,1024]{4,3,2,1,0:T(2,128)(2,1)} %copy_bitcast_fusion.4), calls=%async_computation.1 | async-start | bytes 1048576 | tf_op jit(solution)/shard_map/all_to_all | solution.py:33
  74.9 12.8 %all-to-all-start.2 = ((f32[16,1,4096]{2,1,0:T(1,128)}), f32[16,1,4096]{2,1,0:T(1,128)S(1)}, u32[]{:S(2)}, u32[]{:S(2)}) async-start(f32[16,1,4096]{2,1,0:T(1,128)} %reshape.34), calls=%async_computation.2 | async-start | bytes 524288 | tf_op jit(solution)/shard_map/all_to_all | solution.py:93
  80.0 23.7 %copy-start.1 = (f32[1024]{0:T(1024)S(1)}, f32[1024]{0:T(1024)}, u32[]{:S(2)}) copy-start(f32[1024]{0:T(1024)} %param.7) | copy-start | bytes 12292
  103.9 12.4 %collective-permute-start = (bf16[26,2,1]{2,1,0:T(2,128)(2,1)S(1)}, bf16[26,2,1]{2,1,0:T(2,128)(2,1)S(1)}, u32[]{:S(2)}, u32[]{:S(2)}) collective-permute-start(bf16[26,2,1]{2,1,0:T(2,128)(2,1)S(1)} %get-tuple-element.10), channel_id=1, source_target_pairs={{0,4},{4,8},{8,12},{1,5},{5,9},{9,13},{2,6},{6,10},{10,14},{3,7},{... | collective-permute-start | bytes 320 | tf_op jit(solution)/shard_map/ppermute | solution.py:45
  114.4 8.9 %collective-permute-start.1 = (bf16[26,2,1]{2,1,0:T(2,128)(2,1)S(1)}, bf16[26,2,1]{2,1,0:T(2,128)(2,1)S(1)}, u32[]{:S(2)}, u32[]{:S(2)}) collective-permute-start(bf16[26,2,1]{2,1,0:T(2,128)(2,1)S(1)} %get-tuple-element.9), channel_id=1, source_target_pairs={{4,0},{8,4},{12,8},{5,1},{9,5},{13,9},{6,2},{10,6},{14,10},{7,3},{... | collective-permute-start | bytes 320 | tf_op jit(solution)/shard_map/ppermute | solution.py:47
